TPU v7x, 128 devices: a whole 4x4x4 slice. The times are simulated.
128 devices in a mesh: row: 8 (over z, x_lo), col: 16 (over x_hi, y, core).
Axes of the slice: x: 4 (x_hi: 2, x_lo: 2; x = x_hi * 2 + x_lo), y: 4, z: 4, core: 2. Of those that a mesh axis runs over, the one named last changes fastest.
Arguments:
- occupations: int32 [8192, 128], P('row'), may hold values from 0 to 2
- table: float32 [384, 1024], replicated, may hold values from -0.5 to 0.5
- weights: float32 [2, 1024, 4096], P(None, None, 'col'), may hold values from -0.1875 to 0.1875
- biases: float32 [2, 4096], P(None, 'col'), may hold values from -6 to 6
- heads: float32 [2, 4096], P(None, 'col'), may hold values from -18 to 18
- energies: float32 [8192], P('row'), may hold values from -6 to 6
Outputs:
- schur: float32 [8192, 8192], P('row', 'col')
- solved_rhs: float32 [8192], P('row')
All inputs are finite; a program needn't handle non-finite values.
Results may differ from a plain program's by a relative error of at most 0.0034.
Values may be sent and summed in bfloat16 or wider, within the bound.
No kernel may reach another device: no remote copies, remote signals or barrier semaphores. Data moves between devices by JAX's collectives and lax.ppermute only.
A program may use at most 128 MiB of HBM per device.

v0:
```python
import functools
import math
import jax
import jax.numpy as jnp
from jax import lax
from jax.sharding import Mesh
from jax.sharding import PartitionSpec as P

ROW = ("row_0", "row_1")
norm_eps = 1e-06
diag_shift = 0.05


def over_axes(shard, axes):
    return functools.reduce(lax.psum, axes, shard)


def rows_for(lines, devices):
    spare = -len(lines) % devices
    return jnp.pad(lines, [(0, spare)] + [(0, 0)] * (lines.ndim - 1))


def broadcast_by_parts(shard, axis, root):
    lines = jnp.where(lax.axis_index(axis) == root, shard, jnp.zeros_like(shard)).reshape(
        -1, *shard.shape[1:][-1:]
    )
    padded = rows_for(lines, lax.axis_size(axis))
    own = lax.psum_scatter(padded, axis, scatter_dimension=0, tiled=True)
    return lax.all_gather(own, axis, axis=0, tiled=True)[: len(lines)].reshape(shard.shape)


def broadcast(block, axis, holder):
    block = jnp.where(lax.axis_index(axis) == holder, block, jnp.zeros_like(block))
    return lax.psum(block, axis)


def jacobian(occupations, table, weights, biases, heads):
    onehot = jnp.concatenate(
        [
            (occupations == 0).astype(jnp.float32),
            (occupations == 1).astype(jnp.float32),
            (occupations == 2).astype(jnp.float32),
        ],
        axis=1,
    )
    embedded = jnp.dot(
        onehot, table, precision=lax.Precision.HIGHEST, preferred_element_type=jnp.float32
    )
    embedded = embedded * lax.rsqrt(
        jnp.mean(embedded * embedded, axis=-1, keepdims=True) + norm_eps
    )
    blocks = []
    for panel_index in range(2):
        hidden = (
            jnp.dot(
                embedded,
                weights[panel_index],
                precision=lax.Precision.HIGHEST,
                preferred_element_type=jnp.float32,
            )
            + biases[panel_index]
        )
        blocks.append(heads[panel_index] * jax.nn.sigmoid(hidden))
    return jnp.concatenate(blocks, axis=1)


def on_device(occupations, table, weights, biases, heads, energies):
    row_count = occupations.shape[0]
    row_devices = lax.axis_size(ROW)
    col_devices = lax.axis_size("col")
    sample_total = row_count * row_devices
    panel_width = sample_total // col_devices
    derivs = jacobian(occupations, table, weights, biases, heads)
    col_sums = over_axes(jnp.sum(derivs, axis=0), ROW)
    centered = ((derivs - col_sums / sample_total) * (1.0 / math.sqrt(sample_total))).astype(
        jnp.bfloat16
    )
    own_rows = lax.all_gather(centered, "col", axis=1, tiled=True)
    every_sample = lax.all_gather(centered, ROW, axis=0, tiled=True)
    partner = lax.all_to_all(every_sample, "col", split_axis=0, concat_axis=1, tiled=True)
    kernel = lax.dot_general(
        own_rows, partner, (((1,), (1,)), ((), ())), preferred_element_type=jnp.float32
    )
    row_ids = lax.axis_index(ROW) * row_count + lax.iota(jnp.int32, row_count)
    col_ids = lax.axis_index("col") * panel_width + lax.iota(jnp.int32, panel_width)
    kernel = kernel + jnp.where(row_ids[:, None] == col_ids[None, :], diag_shift, 0.0).astype(
        jnp.float32
    )
    right_side = energies
    for panel_index in range(2):
        start_global = panel_index * panel_width
        root_row = start_global // row_count
        offset = start_global % row_count
        top_block, top_side = (
            broadcast_by_parts(kernel[offset : offset + panel_width], ROW, root_row),
            broadcast_by_parts(right_side[offset : offset + panel_width], ROW, root_row),
        )
        column, diag_block = (
            broadcast(kernel, "col", panel_index),
            broadcast(top_block, "col", panel_index),
        )
        factor = jnp.linalg.cholesky(diag_block)
        left_rows = lax.linalg.triangular_solve(
            factor, column, left_side=False, lower=True, transpose_a=True
        )
        right_rows = lax.linalg.triangular_solve(
            factor, top_block.T, left_side=False, lower=True, transpose_a=True
        )
        kernel = kernel - lax.dot_general(
            left_rows,
            right_rows,
            (((1,), (1,)), ((), ())),
            precision=lax.Precision.HIGHEST,
            preferred_element_type=jnp.float32,
        )
        solved = lax.linalg.triangular_solve(factor, top_side[:, None], left_side=True, lower=True)[
            :, 0
        ]
        right_side = right_side - jnp.dot(
            left_rows, solved, precision=lax.Precision.HIGHEST, preferred_element_type=jnp.float32
        )
        placed = right_side.at[offset : offset + panel_width].set(solved)
        right_side = jnp.where(lax.axis_index(ROW) == root_row, placed, right_side)
    return (kernel, right_side)


def solution(mesh):
    torus = Mesh(mesh.devices.reshape(4, 2, mesh.shape["col"]), ("row_0", "row_1", "col"))
    placed = (P(ROW, None), P(), P(None, None, "col"), P(None, "col"), P(None, "col"), P(ROW))
    return jax.shard_map(
        on_device, mesh=torus, in_specs=placed, out_specs=(P(ROW, "col"), P(ROW)), check_vma=False
    )
```

profile of v0, /device:TPU:1, one launch (start us, length us, event | category | flops | bytes accessed | tf_op | source)
XLA Modules:
  0.0 1241.6 jit_solution(15039333910361492338)
XLA Ops:
  21.2 10.6 psum.42
  37.5 169.9 %all-gather.7.cloned.1.call-done = bf16[8192,512]{0,1:T(8,128)(2,1)} async-done(((bf16[1024,512]{0,1:T(8,128)(2,1)}), bf16[8192,512]{0,1:T(8,128)(2,1)}) %all-gather.7.cloned.1.call-update) | async-done | bytes 8388624 | tf_op jit(solution)/shard_map/all_gather | solution.py:79
  222.3 137.7 %all-to-all-done = bf16[16,512,512]{1,2,0:T(8,128)(2,1)} async-done(((bf16[16,512,512]{1,2,0:T(8,128)(2,1)}), bf16[16,512,512]{1,2,0:T(8,128)(2,1)}, u32[]{:S(2)}, u32[]{:S(2)}) %all-to-all-start) | async-done | bytes 8388640 | tf_op jit(solution)/shard_map/all_to_all | solution.py:80
  360.0 54.5 %all-gather.5.cloned.1.call-done = bf16[1024,8192]{0,1:T(8,128)(2,1)} async-done(((bf16[1024,512]{0,1:T(8,128)(2,1)}), bf16[1024,8192]{0,1:T(8,128)(2,1)}) %all-gather.5.cloned.1.call-update) | async-done | bytes 16777232 | tf_op jit(solution)/shard_map/all_gather | solution.py:78
  414.5 15.9 %broadcast_select_fusion.1 = (f32[1024,512]{0,1:T(8,128)}, f32[1024,512]{0,1:T(8,128)S(1)}) fusion(pred[]{:T(512)S(6)} %eq.56, s32[512]{0:T(512)S(1)} %iota_add_fusion.1, s32[1024]{0:T(1024)S(1)} %iota_add_fusion, bf16[1024,8192]{0,1:T(8,128)(2,1)} %all-gather.5.cloned.1.call-done, bf16[512,8192]{0,1:T(8,128)(2,1)} %bitcast.7), kind=kOutput, calls=%fused_computation.126 | convolution fusion | flops 8592031744 | bytes 29366272 | tf_op jit(solution)/shard_map/dot_general | solution.py:81
  433.2 36.6 %reduce-scatter.7.cloned.1.call-done = f32[64,512]{1,0:T(8,128)} async-done(((f32[512,512]{1,0:T(8,128)}), f32[64,512]{1,0:T(8,128)}) %reduce-scatter.7.cloned.1.call-update) | async-done | bytes 131088 | tf_op jit(solution)/shard_map/reduce_scatter | solution.py:28
  469.9 40.9 %all-gather.9.cloned.1.call-done = f32[512,512]{1,0:T(8,128)} async-done(((f32[64,512]{1,0:T(8,128)}), f32[512,512]{1,0:T(8,128)}) %all-gather.9.cloned.1.call-update) | async-done | bytes 1048592 | tf_op jit(solution)/shard_map/all_gather | solution.py:29
  513.8 151.1 %all-reduce.12.cloned.1.call-done = (f32[1024,512]{0,1:T(8,128)}, f32[512,512]{0,1:T(8,128)}) async-done(((f32[1024,512]{0,1:T(8,128)}, f32[512,512]{0,1:T(8,128)}), (f32[1024,512]{0,1:T(8,128)}, f32[512,512]{0,1:T(8,128)})) %all-reduce.12.cloned.1.call-update) | async-done | bytes 3145744 | tf_op jit(solution)/shard_map/psum | solution.py:34
  669.9 11.7 cholesky.286
  681.8 9.8 custom-call.35
  694.2 11.7 cholesky.305
  705.9 10.2 custom-call.36
  717.7 11.7 cholesky.326
  730.1 9.8 custom-call.37
  741.4 11.7 cholesky.343
  758.4 11.4 while.14
  769.8 39.3 %custom-call.38 = f32[4,128,128]{1,2,0:T(8,128)S(1)} custom-call(f32[4,128,128]{2,1,0:T(8,128)S(1)} %get-tuple-element.72), custom_call_target="InvertDiagBlocksLowerTriangular" | custom-call | tf_op jit(solution)/shard_map/triangular_solve/custom-call.3 | solution.py:103
  829.5 38.3 %reduce-scatter.9.cloned.1.call-done = f32[64,512]{1,0:T(8,128)} async-done(((f32[512,512]{1,0:T(8,128)}), f32[64,512]{1,0:T(8,128)}) %reduce-scatter.9.cloned.1.call-update) | async-done | bytes 131088 | tf_op jit(solution)/shard_map/reduce_scatter | solution.py:28
  867.8 41.0 %all-gather.11.cloned.1.call-done = f32[512,512]{1,0:T(8,128)} async-done(((f32[64,512]{1,0:T(8,128)}), f32[512,512]{1,0:T(8,128)}) %all-gather.11.cloned.1.call-update) | async-done | bytes 1048592 | tf_op jit(solution)/shard_map/all_gather | solution.py:29
  914.0 14.5 %all-reduce.3 = f32[512]{0:T(512)S(1)} all-reduce(f32[512]{0:T(512)S(1)} %slice_select_fusion.3), channel_id=4, replica_groups=mesh['row_0'=4,'row_1'=2,'col'=16] {'row_0','row_1'}, use_global_device_ids=true, to_apply=%region_18.22.clone | all-reduce | flops 512 | bytes 4096
  928.7 12.9 %all-reduce.1 = f32[512]{0:T(512)S(1)} all-reduce(f32[512]{0:T(512)S(1)} %dynamic-slice_dynamic-update-slice_fusion.1), channel_id=1, replica_groups=mesh['row_0'=4,'row_1'=2,'col'=16] {'row_0','row_1'}, use_global_device_ids=true, to_apply=%add.1 | all-reduce | flops 512 | bytes 4096
  945.5 14.7 %all-reduce.4 = f32[512]{0:T(512)S(1)} all-reduce(f32[512]{0:T(512)S(1)} %slice_select_fusion.2), channel_id=5, replica_groups=mesh['row_0'=4,'row_1'=2,'col'=16] {'row_0','row_1'}, use_global_device_ids=true, to_apply=%region_19.24.clone | all-reduce | flops 512 | bytes 4096
  960.4 13.8 %all-reduce.2 = f32[512]{0:T(512)S(1)} all-reduce(f32[512]{0:T(512)S(1)} %dynamic-slice_dynamic-update-slice_fusion), channel_id=1, replica_groups=mesh['row_0'=4,'row_1'=2,'col'=16] {'row_0','row_1'}, use_global_device_ids=true, to_apply=%add.2 | all-reduce | flops 512 | bytes 4096
  974.2 89.2 %all-reduce.10.cloned.1.call-done = (f32[1024,512]{0,1:T(8,128)}, f32[512,512]{0,1:T(8,128)}) async-done(((f32[1024,512]{0,1:T(8,128)}, f32[512,512]{0,1:T(8,128)}), (f32[1024,512]{0,1:T(8,128)}, f32[512,512]{0,1:T(8,128)})) %all-reduce.10.cloned.1.call-update) | async-done | bytes 3145744 | tf_op jit(solution)/shard_map/psum | solution.py:34
  1068.5 11.7 cholesky.358
  1080.4 9.8 custom-call.40
  1092.7 11.7 cholesky.377
  1105.8 10.0 custom-call.41
  1117.3 11.7 cholesky.398
  1141.1 11.7 cholesky.415
  1157.3 11.4 while.15
  1168.7 39.3 %custom-call.43 = f32[4,128,128]{1,2,0:T(8,128)S(1)} custom-call(f32[4,128,128]{2,1,0:T(8,128)S(1)} %get-tuple-element.74), custom_call_target="InvertDiagBlocksLowerTriangular" | custom-call | tf_op jit(solution)/shard_map/triangular_solve/custom-call.3 | solution.py:103
  (213 shorter events, 156.1 us)
Async XLA Ops:
  7.2 1.6 copy-start
  7.2 200.3 %all-gather.7.cloned.1.call-start = ((), (), s32[]{:S(2)}) async-start(), calls=%async_computation.4 | async-start | bytes 9437184 | tf_op jit(solution)/shard_map/all_gather | solution.py:79
  8.7 3.7 copy-start.19
  8.7 3.7 copy-start.20
  8.7 3.7 copy-start.21
  36.8 377.7 %all-gather.5.cloned.1.call-start = ((), (), s32[]{:S(2)}) async-start(), calls=%async_computation.3 | async-start | bytes 17825792 | tf_op jit(solution)/shard_map/all_gather | solution.py:78
  214.9 145.1 %all-to-all-start = ((bf16[16,512,512]{1,2,0:T(8,128)(2,1)}), bf16[16,512,512]{1,2,0:T(8,128)(2,1)}, u32[]{:S(2)}, u32[]{:S(2)}) async-start(bf16[16,512,512]{1,2,0:T(8,128)(2,1)} %bitcast.258), calls=%async_computation | async-start | bytes 16777216 | tf_op jit(solution)/shard_map/all_to_all | solution.py:80
  222.2 247.7 %reduce-scatter.7.cloned.1.call-start = ((), (), s32[]{:S(2)}) async-start(), calls=%async_computation.7 | async-start | bytes 1179648 | tf_op jit(solution)/shard_map/reduce_scatter | solution.py:28
  430.4 1.4 copy-start.6
  433.1 77.7 %all-gather.9.cloned.1.call-start = ((), (), s32[]{:S(2)}) async-start(), calls=%async_computation.5 | async-start | bytes 1179648 | tf_op jit(solution)/shard_map/all_gather | solution.py:29
  469.9 195.0 %all-reduce.12.cloned.1.call-start = ((), (), s32[]{:S(2)}) async-start(), calls=%async_computation.10 | async-start | bytes 6291456 | tf_op jit(solution)/shard_map/psum | solution.py:34
  513.5 354.2 %reduce-scatter.9.cloned.1.call-start = ((), (), s32[]{:S(2)}) async-start(), calls=%async_computation.8 | async-start | bytes 1179648 | tf_op jit(solution)/shard_map/reduce_scatter | solution.py:28
  664.9 2.6 copy-start.10
  669.0 1.0 copy-start.12
  769.8 43.5 %copy-start.4 = (f32[512,512]{1,0:T(8,128)S(1)}, f32[512,512]{1,0:T(8,128)}, u32[]{:S(2)}) copy-start(f32[512,512]{1,0:T(8,128)} %get-tuple-element.260) | copy-start | bytes 3145732
  809.1 4.2 copy-start.15
  814.6 6.6 copy-start.8
  816.4 4.8 copy-start.13
  817.5 3.8 copy-start.7
  826.6 1.4 copy-start.2
  829.4 79.4 %all-gather.11.cloned.1.call-start = ((), (), s32[]{:S(2)}) async-start(), calls=%async_computation.6 | async-start | bytes 1179648 | tf_op jit(solution)/shard_map/all_gather | solution.py:29
  867.8 195.7 %all-reduce.10.cloned.1.call-start = ((), (), s32[]{:S(2)}) async-start(), calls=%async_computation.9 | async-start | bytes 6291456 | tf_op jit(solution)/shard_map/psum | solution.py:34
  911.5 0.7 copy-start.18
  911.5 2.5 copy-start.16
  1063.5 2.6 copy-start.9
  1067.5 1.0 copy-start.11
  1210.5 5.8 copy-start.5
  1210.5 5.8 copy-start.14
  1221.8 3.8 copy-start.3
  1225.6 8.8 copy-start.1
  1233.8 0.6 copy-start.17
Sparse Core Ops, SparseCore 0:
  36.9 170.4 all-gather.6
  210.5 203.9 all-gather.4
  433.3 36.5 reduce-scatter.6
  471.3 39.4 all-gather.8
  513.8 151.0 all-reduce.11
  829.6 38.1 reduce-scatter.8
  869.4 39.4 all-gather.10
  912.0 151.3 all-reduce.9
where the time goes:
time: 1250 us; the launch traced here: 1240 us
  waiting for transfers between devices  760 us (61%)
  other arithmetic  247 us (20%)
  matrix products  82.7 us (7%)
  blocking collectives  70.3 us (6%)
  local copies, waits for them, and re-layouts  51.3 us (4%)
  between operations  21.7 us (2%)
    psum x2, waiting for transfers between devices, broadcast(): return lax.psum(block, axis)  240 us
    all_gather x1, waiting for transfers between devices, on_device(): every_sample = lax.all_gather(centered, ROW, axis=0, tiled=True)  170 us
    another operation x29, other arithmetic, on_device(): factor = jnp.linalg.cholesky(diag_block)  158 us
    all_to_all x1, waiting for transfers between devices, on_device(): lax.all_to_all(every_sample, 'col', split_axis=0, concat_axis=1, tiled=True)  138 us
    all_gather x2, waiting for transfers between devices, broadcast_by_parts(): lax.all_gather(own, axis, axis=0, tiled=True)[:len(lines)]  81.9 us
    another operation x5, other arithmetic, on_device(): lax.linalg.triangular_solve(factor, column, left_side=False, lower=True,...  81.2 us
    reduce_scatter x2, waiting for transfers between devices, broadcast_by_parts(): own = lax.psum_scatter(padded, axis, scatter_dimension=0, tiled=True)  74.9 us
    unnamed x4, blocking collectives  56 us
  transfers between devices with their start and end apart: 9, of which 9 were waited for; matrix products, arithmetic and copies ran while one was open for 1% of the time, Pallas kernels for 0%

commit v1 on v0

--- a/solution.py
+++ b/solution.py
@@ -76,7 +76,9 @@
         jnp.bfloat16
     )
     own_rows = lax.all_gather(centered, "col", axis=1, tiled=True)
-    every_sample = lax.all_gather(centered, ROW, axis=0, tiled=True)
+    v_next = jnp.stack([centered] * jax.lax.axis_size(ROW))
+    newest = jax.lax.all_to_all(v_next, ROW, split_axis=0, concat_axis=0)
+    every_sample = jnp.concatenate(newest, 0)
     partner = lax.all_to_all(every_sample, "col", split_axis=0, concat_axis=1, tiled=True)
     kernel = lax.dot_general(
         own_rows, partner, (((1,), (1,)), ((), ())), preferred_element_type=jnp.float32

time: 1250 us -> 1180 us (0.944)
  waiting for transfers between devices: 760 us -> 524 us
  blocking collectives: 70.3 us -> 221 us
    all_gather x1 -> x0, waiting for transfers between devices: 170 us -> none  [on_device(): every_sample = lax.all_gather(centered, ROW, axis=0, tiled=True)]
    all_to_all x0 -> x1, blocking collectives: none -> 151 us  [on_device(): newest = jax.lax.all_to_all(v_next, ROW, split_axis=0, concat_axis=0)]
    all_gather x1, waiting for transfers between devices: 54.5 us -> 0.01 us  [on_device(): own_rows = lax.all_gather(centered, 'col', axis=1, tiled=True)]
    all_to_all x1, waiting for transfers between devices: 138 us -> 120 us  [on_device(): lax.all_to_all(every_sample, 'col', split_axis=0, concat_axis=1, tiled=True)]
  transfers between devices with their start and end apart: 9 -> 8, of which waited for: 9 -> 7; matrix products, arithmetic and copies ran while one was open for 1% -> 2% of each run, Pallas kernels for 0% -> 0%
where the time goes in v1:
time: 1180 us; the launch traced here: 1170 us
  waiting for transfers between devices  524 us (44%)
  other arithmetic  247 us (21%)
  blocking collectives  221 us (19%)
  matrix products  82.7 us (7%)
  local copies, waits for them, and re-layouts  58.4 us (5%)
  between operations  21.7 us (2%)
  starting transfers between devices  12.1 us (1%)
    psum x2, waiting for transfers between devices, broadcast(): return lax.psum(block, axis)  240 us
    another operation x29, other arithmetic, on_device(): factor = jnp.linalg.cholesky(diag_block)  158 us
    all_to_all x1, blocking collectives, on_device(): newest = jax.lax.all_to_all(v_next, ROW, split_axis=0, concat_axis=0)  151 us
    all_to_all x1, waiting for transfers between devices, on_device(): lax.all_to_all(every_sample, 'col', split_axis=0, concat_axis=1, tiled=True)  120 us
    all_gather x2, waiting for transfers between devices, broadcast_by_parts(): lax.all_gather(own, axis, axis=0, tiled=True)[:len(lines)]  81.9 us
    reduce_scatter x2, waiting for transfers between devices, broadcast_by_parts(): own = lax.psum_scatter(padded, axis, scatter_dimension=0, tiled=True)  81.5 us
    another operation x5, other arithmetic, on_device(): lax.linalg.triangular_solve(factor, column, left_side=False, lower=True,...  81.2 us
    unnamed x4, blocking collectives  56 us
  transfers between devices with their start and end apart: 8, of which 7 were waited for; matrix products, arithmetic and copies ran while one was open for 2% of the time, Pallas kernels for 0%

profile of v1, /device:TPU:1, one launch (start us, length us, event | category | flops | bytes accessed | tf_op | source)
XLA Modules:
  0.0 1167.3 jit_solution(15369498677767221358)
XLA Ops:
  21.2 10.6 psum.42
  39.0 150.7 %all_to_all.24 = bf16[8,1024,512]{2,1,0:T(8,128)(2,1)} all-to-all(bf16[8,1024,512]{2,1,0:T(8,128)(2,1)S(1)} %stack.2), channel_id=1, replica_groups=mesh['row_0'=4,'row_1'=2,'col'=16] {'row_0','row_1'}, dimensions={0} | all-to-all | bytes 16777216 | tf_op jit(solution)/shard_map/all_to_all | solution.py:80
  189.7 11.7 all-to-all-start.1
  201.4 119.9 %all-to-all-done.1 = bf16[16,512,512]{2,1,0:T(8,128)(2,1)} async-done(((bf16[16,512,512]{2,1,0:T(8,128)(2,1)}), bf16[16,512,512]{2,1,0:T(8,128)(2,1)}, u32[]{:S(2)}, u32[]{:S(2)}) %all-to-all-start.1) | async-done | bytes 8388640 | tf_op jit(solution)/shard_map/all_to_all | solution.py:82
  321.3 12.3 %copy.37 = bf16[512,16,512]{0,2,1:T(8,128)(2,1)} copy(bf16[512,16,512]{2,0,1:T(8,128)(2,1)} %bitcast.7) | data formatting | bytes 16777216 | tf_op jit(solution)/shard_map/all_to_all | solution.py:82
  333.6 15.9 %broadcast_select_fusion.1 = (f32[1024,512]{0,1:T(8,128)}, f32[1024,512]{0,1:T(8,128)S(1)}) fusion(pred[]{:T(512)S(6)} %eq.56, s32[512]{0:T(512)S(1)} %iota_add_fusion.1, s32[1024]{0:T(1024)S(1)} %iota_add_fusion, bf16[1024,8192]{0,1:T(8,128)(2,1)} %all-gather.4.cloned.1.call-done, bf16[512,8192]{0,1:T(8,128)(2,1)} %bitcast.271), kind=kOutput, calls=%fused_computation.125 | convolution fusion | flops 8592031744 | bytes 29366272 | tf_op jit(solution)/shard_map/dot_general | solution.py:83
  352.3 43.2 %reduce-scatter.7.cloned.1.call-done = f32[64,512]{1,0:T(8,128)} async-done(((f32[512,512]{1,0:T(8,128)}), f32[64,512]{1,0:T(8,128)}) %reduce-scatter.7.cloned.1.call-update) | async-done | bytes 131088 | tf_op jit(solution)/shard_map/reduce_scatter | solution.py:28
  395.6 41.0 %all-gather.6.cloned.1.call-done = f32[512,512]{1,0:T(8,128)} async-done(((f32[64,512]{1,0:T(8,128)}), f32[512,512]{1,0:T(8,128)}) %all-gather.6.cloned.1.call-update) | async-done | bytes 1048592 | tf_op jit(solution)/shard_map/all_gather | solution.py:29
  439.6 151.1 %all-reduce.12.cloned.1.call-done = (f32[1024,512]{0,1:T(8,128)}, f32[512,512]{0,1:T(8,128)}) async-done(((f32[1024,512]{0,1:T(8,128)}, f32[512,512]{0,1:T(8,128)}), (f32[1024,512]{0,1:T(8,128)}, f32[512,512]{0,1:T(8,128)})) %all-reduce.12.cloned.1.call-update) | async-done | bytes 3145744 | tf_op jit(solution)/shard_map/psum | solution.py:34
  595.8 11.7 %cholesky.286 = f32[128,128]{1,0:T(8,128)S(1)} custom-call(f32[128,128]{1,0:T(8,128)S(1)} %cholesky.426), custom_call_target="Cholesky" | custom-call | tf_op jit(solution)/shard_map/jit(cholesky)/cholesky | solution.py:104
  607.7 9.8 custom-call.35
  620.0 11.7 %cholesky.305 = f32[128,128]{1,0:T(8,128)S(1)} custom-call(f32[128,128]{1,0:T(8,128)S(1)} %cholesky.430), custom_call_target="Cholesky" | custom-call | tf_op jit(solution)/shard_map/jit(cholesky)/cholesky | solution.py:104
  631.8 10.2 custom-call.36
  643.6 11.7 %cholesky.326 = f32[128,128]{1,0:T(8,128)S(1)} custom-call(f32[128,128]{1,0:T(8,128)S(1)} %cholesky.435), custom_call_target="Cholesky" | custom-call | tf_op jit(solution)/shard_map/jit(cholesky)/cholesky | solution.py:104
  667.2 11.7 %cholesky.343 = f32[128,128]{1,0:T(8,128)S(1)} custom-call(f32[128,128]{1,0:T(8,128)S(1)} %convolution_subtract_fusion.17), custom_call_target="Cholesky" | custom-call | tf_op jit(solution)/shard_map/jit(cholesky)/cholesky | solution.py:104
  684.2 11.4 while.14
  695.6 39.3 %custom-call.38 = f32[4,128,128]{1,2,0:T(8,128)S(1)} custom-call(f32[4,128,128]{2,1,0:T(8,128)S(1)} %get-tuple-element.72), custom_call_target="InvertDiagBlocksLowerTriangular" | custom-call | tf_op jit(solution)/shard_map/triangular_solve/custom-call.3 | solution.py:105
  755.3 38.3 %reduce-scatter.9.cloned.1.call-done = f32[64,512]{1,0:T(8,128)} async-done(((f32[512,512]{1,0:T(8,128)}), f32[64,512]{1,0:T(8,128)}) %reduce-scatter.9.cloned.1.call-update) | async-done | bytes 131088 | tf_op jit(solution)/shard_map/reduce_scatter | solution.py:28
  793.7 40.9 %all-gather.8.cloned.1.call-done = f32[512,512]{1,0:T(8,128)} async-done(((f32[64,512]{1,0:T(8,128)}), f32[512,512]{1,0:T(8,128)}) %all-gather.8.cloned.1.call-update) | async-done | bytes 1048592 | tf_op jit(solution)/shard_map/all_gather | solution.py:29
  839.7 14.5 %all-reduce.3 = f32[512]{0:T(512)S(1)} all-reduce(f32[512]{0:T(512)S(1)} %slice_select_fusion.3), channel_id=4, replica_groups=mesh['row_0'=4,'row_1'=2,'col'=16] {'row_0','row_1'}, use_global_device_ids=true, to_apply=%region_18.22.clone | all-reduce | flops 512 | bytes 4096
  854.4 12.9 %all-reduce.1 = f32[512]{0:T(512)S(1)} all-reduce(f32[512]{0:T(512)S(1)} %dynamic-slice_dynamic-update-slice_fusion.1), channel_id=1, replica_groups=mesh['row_0'=4,'row_1'=2,'col'=16] {'row_0','row_1'}, use_global_device_ids=true, to_apply=%add.1 | all-reduce | flops 512 | bytes 4096
  871.2 14.7 %all-reduce.4 = f32[512]{0:T(512)S(1)} all-reduce(f32[512]{0:T(512)S(1)} %slice_select_fusion.2), channel_id=5, replica_groups=mesh['row_0'=4,'row_1'=2,'col'=16] {'row_0','row_1'}, use_global_device_ids=true, to_apply=%region_19.24.clone | all-reduce | flops 512 | bytes 4096
  886.1 13.8 %all-reduce.2 = f32[512]{0:T(512)S(1)} all-reduce(f32[512]{0:T(512)S(1)} %dynamic-slice_dynamic-update-slice_fusion), channel_id=1, replica_groups=mesh['row_0'=4,'row_1'=2,'col'=16] {'row_0','row_1'}, use_global_device_ids=true, to_apply=%add.2 | all-reduce | flops 512 | bytes 4096
  899.9 89.2 %all-reduce.10.cloned.1.call-done = (f32[1024,512]{0,1:T(8,128)}, f32[512,512]{0,1:T(8,128)}) async-done(((f32[1024,512]{0,1:T(8,128)}, f32[512,512]{0,1:T(8,128)}), (f32[1024,512]{0,1:T(8,128)}, f32[512,512]{0,1:T(8,128)})) %all-reduce.10.cloned.1.call-update) | async-done | bytes 3145744 | tf_op jit(solution)/shard_map/psum | solution.py:34
  994.2 11.7 %cholesky.358 = f32[128,128]{1,0:T(8,128)S(1)} custom-call(f32[128,128]{1,0:T(8,128)S(1)} %cholesky.439), custom_call_target="Cholesky" | custom-call | tf_op jit(solution)/shard_map/jit(cholesky)/cholesky | solution.py:104
  1006.1 9.8 custom-call.40
  1018.4 11.7 %cholesky.377 = f32[128,128]{1,0:T(8,128)S(1)} custom-call(f32[128,128]{1,0:T(8,128)S(1)} %cholesky.443), custom_call_target="Cholesky" | custom-call | tf_op jit(solution)/shard_map/jit(cholesky)/cholesky | solution.py:104
  1031.5 10.0 custom-call.41
  1043.0 11.7 %cholesky.398 = f32[128,128]{1,0:T(8,128)S(1)} custom-call(f32[128,128]{1,0:T(8,128)S(1)} %cholesky.448), custom_call_target="Cholesky" | custom-call | tf_op jit(solution)/shard_map/jit(cholesky)/cholesky | solution.py:104
  1066.8 11.7 %cholesky.415 = f32[128,128]{1,0:T(8,128)S(1)} custom-call(f32[128,128]{1,0:T(8,128)S(1)} %convolution_subtract_fusion.16), custom_call_target="Cholesky" | custom-call | tf_op jit(solution)/shard_map/jit(cholesky)/cholesky | solution.py:104
  1083.0 11.4 while.15
  1094.4 39.3 %custom-call.43 = f32[4,128,128]{1,2,0:T(8,128)S(1)} custom-call(f32[4,128,128]{2,1,0:T(8,128)S(1)} %get-tuple-element.74), custom_call_target="InvertDiagBlocksLowerTriangular" | custom-call | tf_op jit(solution)/shard_map/triangular_solve/custom-call.3 | solution.py:105
  (213 shorter events, 152.6 us)
Async XLA Ops:
  7.2 1.6 copy-start
  7.2 326.5 %all-gather.4.cloned.1.call-start = ((), (), s32[]{:S(2)}) async-start(), calls=%async_computation.4 | async-start | bytes 17825792 | tf_op jit(solution)/shard_map/all_gather | solution.py:78
  8.7 3.7 copy-start.19
  8.7 3.7 copy-start.20
  8.7 3.7 copy-start.21
  189.7 131.6 %all-to-all-start.1 = ((bf16[16,512,512]{2,1,0:T(8,128)(2,1)}), bf16[16,512,512]{2,1,0:T(8,128)(2,1)}, u32[]{:S(2)}, u32[]{:S(2)}) async-start(bf16[16,512,512]{2,1,0:T(8,128)(2,1)} %bitcast.254), calls=%async_computation.1 | async-start | bytes 16777216 | tf_op jit(solution)/shard_map/all_to_all | solution.py:82
  201.3 194.2 %reduce-scatter.7.cloned.1.call-start = ((), (), s32[]{:S(2)}) async-start(), calls=%async_computation.7 | async-start | bytes 1179648 | tf_op jit(solution)/shard_map/reduce_scatter | solution.py:28
  349.5 1.4 copy-start.6
  352.3 84.4 %all-gather.6.cloned.1.call-start = ((), (), s32[]{:S(2)}) async-start(), calls=%async_computation.5 | async-start | bytes 1179648 | tf_op jit(solution)/shard_map/all_gather | solution.py:29
  395.6 195.2 %all-reduce.12.cloned.1.call-start = ((), (), s32[]{:S(2)}) async-start(), calls=%async_computation.10 | async-start | bytes 6291456 | tf_op jit(solution)/shard_map/psum | solution.py:34
  439.4 354.3 %reduce-scatter.9.cloned.1.call-start = ((), (), s32[]{:S(2)}) async-start(), calls=%async_computation.8 | async-start | bytes 1179648 | tf_op jit(solution)/shard_map/reduce_scatter | solution.py:28
  590.7 2.6 copy-start.10
  594.8 1.0 copy-start.12
  695.6 43.5 %copy-start.4 = (f32[512,512]{1,0:T(8,128)S(1)}, f32[512,512]{1,0:T(8,128)}, u32[]{:S(2)}) copy-start(f32[512,512]{1,0:T(8,128)} %get-tuple-element.258) | copy-start | bytes 3145732
  735.0 4.2 copy-start.15
  740.5 6.6 copy-start.8
  742.3 4.8 copy-start.13
  743.3 3.8 copy-start.7
  752.4 1.4 copy-start.2
  755.3 79.3 %all-gather.8.cloned.1.call-start = ((), (), s32[]{:S(2)}) async-start(), calls=%async_computation.6 | async-start | bytes 1179648 | tf_op jit(solution)/shard_map/all_gather | solution.py:29
  793.6 195.5 %all-reduce.10.cloned.1.call-start = ((), (), s32[]{:S(2)}) async-start(), calls=%async_computation.9 | async-start | bytes 6291456 | tf_op jit(solution)/shard_map/psum | solution.py:34
  837.2 0.7 copy-start.18
  837.2 2.5 copy-start.16
  989.2 2.6 copy-start.9
  993.2 1.0 copy-start.11
  1136.2 5.8 copy-start.5
  1136.2 5.8 copy-start.14
  1147.5 3.8 copy-start.3
  1151.3 8.8 copy-start.1
  1159.5 0.6 copy-start.17
Sparse Core Ops, SparseCore 0:
  36.9 168.0 all-gather.3
  352.4 43.0 reduce-scatter.6
  397.2 39.4 all-gather.5
  439.7 151.0 all-reduce.11
  755.4 38.1 reduce-scatter.8
  795.1 39.4 all-gather.7
  837.7 151.3 all-reduce.9
